TPU v7x, 256 devices: a whole 4x4x8 slice. The times are simulated.
256 devices in a mesh: band: 32 (over y, x, core), gslab: 8 (over z).
Axes of the slice: x: 4, y: 4, z: 8, core: 2. Of those that a mesh axis runs over, the one named last changes fastest.
Arguments:
- band_coeffs: float32 [12288, 49152], P('band', 'gslab'), may hold values from -6 to 6
- sign_table: int32 [12, 12288], P(None, 'band'), may hold values from -1 to 1, as said below
- slice_widths: int32 [64], replicated, may hold values from 96 to 384, as said below
- owner_map: int32 [64], replicated, may hold values from 0 to 63, each once
Outputs:
- pseudobands: float32 [768, 49152], P(('band', 'gslab'))
Inputs may be any that keep to these rules, and one draw needn't show every extreme that they name: `sign_table`: every entry is -1 or 1. `slice_widths`: the widths sum to 12288; every slice holds 96 to 384 bands, and in every draw some slice holds exactly 96 and some exactly 384. `owner_map`: each slice appears once.
All inputs are finite; a program needn't handle non-finite values.
Results may differ from a plain program's by a relative error of at most 0.0003.
Values sent between devices are 32-bit elements; how exact they have to be, the bound alone decides.
A program may use at most 128 MiB of HBM per device.

v0:
```python
import jax
import jax.numpy as jnp
from jax import lax
from jax.sharding import PartitionSpec as P


def mixing_rows(row_ids, slice_of_band, sign_float, owner_map, inverse, per_slice):
    slice_count = owner_map.shape[0]
    slot_group = row_ids // per_slice
    within = row_ids % per_slice
    slice_range = jnp.arange(slice_count, dtype=jnp.int32)
    picked = slot_group[:, None] == slice_range[None, :]
    target = jnp.sum(jnp.where(picked, owner_map[None, :], 0), axis=1)
    member = target[:, None] == slice_range[None, :]
    row_scale = jnp.sum(jnp.where(member, inverse[None, :], 0.0), axis=1)
    one_hot = (within[:, None] == jnp.arange(per_slice, dtype=jnp.int32)[None, :]).astype(
        jnp.float32
    )
    sign_rows = jnp.dot(
        one_hot, sign_float, precision=lax.Precision.HIGHEST, preferred_element_type=jnp.float32
    )
    return jnp.where(slice_of_band[None, :] == target[:, None], sign_rows * row_scale[:, None], 0.0)


def on_device(band_coeffs, sign_table, slice_widths, owner_map):
    local_bands = band_coeffs.shape[0]
    per_slice = sign_table.shape[0]
    slice_count = owner_map.shape[0]
    total_rows = slice_count * per_slice
    band_groups = lax.axis_size("band")
    first_band = lax.axis_index("band") * local_bands
    band_ids = first_band + jnp.arange(local_bands, dtype=jnp.int32)
    ends = jnp.cumsum(slice_widths)
    slice_of_band = jnp.sum((band_ids[:, None] >= ends[None, :]).astype(jnp.int32), axis=1)
    inverse = 1.0 / jnp.sqrt(slice_widths.astype(jnp.float32))
    sign_float = sign_table.astype(jnp.float32)
    group_rows = total_rows // band_groups
    row_ids = jnp.arange(group_rows * lax.axis_size("band"), dtype=jnp.int32)
    mixing = mixing_rows(row_ids, slice_of_band, sign_float, owner_map, inverse, per_slice)
    summed = lax.psum_scatter(
        jnp.dot(
            mixing, band_coeffs, precision=lax.Precision.HIGHEST, preferred_element_type=jnp.float32
        ),
        "band",
        scatter_dimension=0,
        tiled=True,
    )
    return lax.all_to_all(summed, "gslab", split_axis=0, concat_axis=1, tiled=True)


def solution(mesh):
    return jax.shard_map(
        on_device,
        mesh=mesh,
        in_specs=(P("band", "gslab"), P(None, "band"), P(), P()),
        out_specs=P(("band", "gslab"), None),
        check_vma=False,
    )
```

profile of v0, /device:TPU:1, one launch (start us, length us, event | category | flops | bytes accessed | tf_op | source)
XLA Modules:
  0.0 212.2 jit_solution(15037606912053290805)
XLA Ops:
  6.5 0.0 reduce-scatter.2.cloned.1.call-start
  6.6 0.7 convert_rsqrt_fusion
  7.2 0.7 copy.8
  8.0 0.1 reduce-window.8
  8.1 0.1 reduce
  8.2 0.8 select_reduce_fusion.1
  8.9 0.1 select_reduce_fusion
  9.1 0.1 convert_reduce_fusion
  9.1 1.4 fusion
  10.6 34.0 %fusion.10 = f32[768,6144]{1,0:T(8,128)} fusion(f32[768,384]{1,0:T(8,128)S(1)} %fusion, f32[384,6144]{1,0:T(8,128)} %param.4), kind=kOutput, calls=%fused_computation.23 | convolution fusion | flops 21743271936 | bytes 29491200 | tf_op jit(solution)/shard_map/dot_general | solution.py:41
  44.6 0.0 reduce-scatter.2.cloned.1.call-update
  44.6 131.8 %reduce-scatter.2.cloned.1.call-done = f32[24,6144]{1,0:T(8,128)} async-done(((f32[768,6144]{1,0:T(8,128)}), f32[24,6144]{1,0:T(8,128)}) %reduce-scatter.2.cloned.1.call-update) | async-done | bytes 589840 | tf_op jit(solution)/shard_map/reduce_scatter | solution.py:40
  176.5 1.3 all_to_all.14
  177.8 26.7 %all_to_all.19 = f32[8,3,6144]{2,1,0:T(4,128)S(1)} all-to-all(f32[8,3,6144]{2,1,0:T(4,128)S(1)} %all_to_all.14), channel_id=1, replica_groups=mesh['band'=32,'gslab'=8] {'gslab'}, dimensions={0} | all-to-all | bytes 1179648 | tf_op jit(solution)/shard_map/all_to_all | solution.py:48
  204.5 0.9 copy.10
  (3 shorter events, 0.0 us)
Async XLA Ops:
  6.5 170.0 %reduce-scatter.2.cloned.1.call-start = ((), (), s32[]{:S(2)}) async-start(), calls=%async_computation.2 | async-start | bytes 19464192 | tf_op jit(solution)/shard_map/reduce_scatter | solution.py:40
Sparse Core Ops, SparseCore 0:
  44.8 131.6 reduce-scatter.1
where the time goes:
time: 214 us; the launch traced here: 212 us
  waiting for transfers between devices  132 us (62%)
  matrix products  35.5 us (17%)
  blocking collectives  26.7 us (12%)
  between operations  13.4 us (6%)
  local copies, waits for them, and re-layouts  2.94 us (1%)
    reduce_scatter x1, waiting for transfers between devices, on_device(): lax.psum_scatter(jnp.dot(mixing, band_coeffs, precision=lax.Precision.HIG...  132 us
    dot_general x1, matrix products, on_device(): jnp.dot(mixing, band_coeffs, precision=lax.Precision.HIGHEST, preferred_e...  34 us
    all_to_all x1, blocking collectives, on_device(): lax.all_to_all(summed, 'gslab', split_axis=0, concat_axis=1, tiled=True)  26.7 us
  transfers between devices with their start and end apart: 1, of which 1 were waited for; matrix products, arithmetic and copies ran while one was open for 0% of the time, Pallas kernels for 0%

commit v1 on v0

v1 whole, which is shorter than its diff:
```python
import jax
import jax.numpy as jnp
from jax import lax
from jax.experimental import pallas as pl
from jax.experimental.pallas import tpu as pltpu
from jax.sharding import PartitionSpec as P

MESH = pl.DeviceIdType.MESH
F32 = jnp.float32
BF16 = jnp.bfloat16

NX, NY, NZ = 4, 4, 8
CHIPS = NX * NY
GROUPS = 2 * CHIPS
BANDS = 384
SLAB = 6144
PHASES = 3
WIDE = SLAB // PHASES
NPS = 12
HALF = 6
SLOTS = 5
ROWS = 32
NSLICE = 64
OUT = NSLICE * HALF

OFFSETS = (
    (1, 0), (0, 1), (3, 0), (0, 3), (1, 1), (3, 3), (1, 3), (3, 1),
    (2, 0), (0, 2), (2, 1), (1, 2), (2, 3), (3, 2), (2, 2),
)


def iota(shape, dim):
    return lax.broadcasted_iota(jnp.int32, shape, dim)


def kernel(
    band_ref, sign_ref, width_ref, owner_ref, out_ref,
    coeffs, sign, width, owner, select, scale,
    a_send, a_recv, z_send, z_recv,
    load_sem, small_sem, a_ssem, a_rsem, z_ssem, z_rsem, b_ssem, b_rsem,
):
    b = lax.axis_index("band")
    g = lax.axis_index("gslab")
    c = lax.rem(b, 2)
    q = b // 2
    x = lax.rem(q, NX)
    y = q // NX

    def chip_at(dx, dy):
        return lax.rem(y + dy, NY) * NX + lax.rem(x + dx, NX)

    loads = [
        pltpu.make_async_copy(band_ref.at[:, pl.ds(p * WIDE, WIDE)], coeffs.at[p], load_sem.at[p])
        for p in range(PHASES)
    ]
    smalls = [
        pltpu.make_async_copy(src, dst, small_sem.at[i])
        for i, (src, dst) in enumerate(((sign_ref, sign), (width_ref, width), (owner_ref, owner)))
    ]
    for copy in smalls:
        copy.start()
    for copy in loads:
        copy.start()

    barrier = pltpu.get_barrier_semaphore()
    greeted = 0
    for dc in range(2):
        for dx, dy in ((0, 0),) + OFFSETS:
            if (dc, dx, dy) != (0, 0, 0):
                peer = chip_at(dx, dy) * 2 + lax.rem(c + dc, 2)
                pl.semaphore_signal(barrier, inc=1, device_id=(peer, g), device_id_type=MESH)
                greeted += 1
        for dz in range(1, NZ):
            peer = q * 2 + lax.rem(c + dc, 2)
            pl.semaphore_signal(
                barrier, inc=1, device_id=(peer, lax.rem(g + dz, NZ)), device_id_type=MESH
            )
            greeted += 1

    for copy in smalls:
        copy.wait()
    width_row = width[...].astype(F32)
    owner_row = owner[...].astype(F32)
    ends = jnp.sum(
        jnp.where(iota((NSLICE, NSLICE), 1) <= iota((NSLICE, NSLICE), 0), width_row, 0.0),
        axis=1, keepdims=True,
    )
    first = b * BANDS
    band_row = (first + iota((1, BANDS), 1)).astype(F32)
    slice_row = jnp.sum(jnp.where(ends <= band_row, 1.0, 0.0), axis=0, keepdims=True)
    first_row = jnp.zeros((1, BANDS), F32) + first.astype(F32)
    first_slice = jnp.sum(jnp.where(ends <= first_row, 1.0, 0.0), axis=0, keepdims=True)
    row = iota((2 * ROWS, BANDS), 0)
    local = row & (ROWS - 1)
    slot = (local * 43) >> 8
    pseudo = (row >> 5) * HALF + local - slot * HALF
    sign_f = sign[...].astype(F32)
    signs = jnp.zeros((2 * ROWS, BANDS), F32)
    for j in range(NPS):
        signs = jnp.where(pseudo == j, sign_f[j : j + 1, :], signs)
    member = (slice_row - first_slice == slot.astype(F32)) & (local < SLOTS * HALF)
    mixing = jnp.where(member, signs, 0.0).astype(BF16)
    mixing = jnp.concatenate([mixing, mixing], axis=1)

    def partial_sums(p):
        loads[p].wait()

        @pl.loop(0, CHIPS // 2)
        def _(pair):
            part = coeffs[p, :, pl.ds(pl.multiple_of(pair * 256, 256), 256)]
            high = part.astype(BF16)
            low = (part - high.astype(F32)).astype(BF16)
            sums = jnp.dot(
                mixing, jnp.concatenate([high, low], axis=0), preferred_element_type=F32
            )
            for side in range(2):
                for half in range(2):
                    a_send[p, pair * 2 + side, half] = sums[
                        half * ROWS : (half + 1) * ROWS, side * 128 : (side + 1) * 128
                    ]

    def a_copy(p, dx, dy, dc):
        chip = chip_at(dx, dy)
        core = lax.rem(c + dc, 2)
        return pltpu.make_async_remote_copy(
            src_ref=a_send.at[p, chip, core],
            dst_ref=a_recv.at[p, b],
            send_sem=a_ssem.at[p],
            recv_sem=a_rsem.at[p],
            device_id=(chip * 2 + core, g),
            device_id_type=MESH,
        )

    def send_a(p):
        for dx, dy in OFFSETS:
            for dc in range(2):
                a_copy(p, dx, dy, dc).start()
        a_copy(p, 0, 0, 1).start()
        a_recv[p, b] = a_send[p, q, c]

    def a_all(p):
        return pltpu.make_async_remote_copy(
            src_ref=a_recv.at[p, pl.ds(0, GROUPS - 1)],
            dst_ref=a_recv.at[p, pl.ds(0, GROUPS - 1)],
            send_sem=a_ssem.at[p],
            recv_sem=a_rsem.at[p],
            device_id=(b, g),
            device_id_type=MESH,
        )

    partial_sums(0)
    pl.semaphore_wait(barrier, greeted)
    send_a(0)
    for p in range(1, PHASES):
        partial_sums(p)
        send_a(p)

    source = iota((1, GROUPS * ROWS), 1)
    source_local = source & (ROWS - 1)
    source_slot = (source_local * 43) >> 8
    source_half = jnp.where(
        source_local < SLOTS * HALF, source_local - source_slot * HALF, -1
    )
    source_first = ((source >> 5) * BANDS).astype(F32)
    source_slice = (
        jnp.sum(jnp.where(ends <= source_first, 1.0, 0.0), axis=0, keepdims=True)
        + source_slot.astype(F32)
    )
    block = OUT // 8
    for e in range(8):
        in_slot, h, cc = e >> 2, (e >> 1) & 1, e & 1
        r = iota((block, NSLICE), 0)
        chip = (r * 43) >> 7
        t = r - chip * 3
        place = (chip * 2 + cc) * 2 + in_slot
        lane = iota((block, NSLICE), 1)
        target = jnp.sum(jnp.where(lane == place, owner_row, 0.0), axis=1, keepdims=True)
        bands = jnp.sum(
            jnp.where(lane.astype(F32) == target, width_row, 0.0), axis=1, keepdims=True
        )
        scale[e * block : (e + 1) * block, :] = jnp.broadcast_to(1.0 / jnp.sqrt(bands), (block, 128))
        r2 = iota((block, GROUPS * ROWS), 0)
        t2 = r2 - ((r2 * 43) >> 7) * 3
        hit = (target == source_slice) & (t2 + 3 * h == source_half)
        select[e * block : (e + 1) * block, :] = jnp.where(hit, 1.0, 0.0).astype(BF16)

    in_class = lax.rem(g, 4) // 2 == c

    def combine(p):
        a_all(p).wait_recv()
        part = a_recv[p].reshape(GROUPS * ROWS, 128)
        high = part.astype(BF16)
        low = (part - high.astype(F32)).astype(BF16)
        both = jnp.dot(
            select[...], jnp.concatenate([high, low], axis=1), preferred_element_type=F32
        )
        rows = (both[:, :128] + both[:, 128:]) * scale[...]
        for e in range(8):
            z_send[p, e] = rows[e * block : (e + 1) * block].reshape(CHIPS, 3, 1, 128)

    def z_copy(p, e):
        plane = (e >> 2) * 4 + 2 * c + ((e >> 1) & 1)
        core = e & 1
        copy = pltpu.make_async_remote_copy(
            src_ref=z_send.at[p, e],
            dst_ref=z_recv.at[p, :, g],
            send_sem=z_ssem.at[p, e],
            recv_sem=z_rsem.at[p, g],
            device_id=(q * 2 + core, plane),
            device_id_type=MESH,
        )
        here = (plane == g) & (core == c)
        return copy, here

    def send_z(p):
        for e in range(8):
            copy, here = z_copy(p, e)

            @pl.when(jnp.logical_not(here))
            def _():
                copy.start()

            @pl.when(here)
            def _():
                z_recv[p, :, g] = z_send[p, e]

    def wait_z(p):
        for plane in range(NZ):
            copy = pltpu.make_async_remote_copy(
                src_ref=z_send.at[p, 0],
                dst_ref=z_recv.at[p, :, plane],
                send_sem=z_ssem.at[p, 0],
                recv_sem=z_rsem.at[p, plane],
                device_id=(b, g),
                device_id_type=MESH,
            )

            @pl.when(jnp.logical_not(in_class & (g == plane)))
            def _():
                copy.wait_recv()

    def b_copy(p, dx, dy):
        chip = chip_at(dx, dy)
        return pltpu.make_async_remote_copy(
            src_ref=z_recv.at[p, chip],
            dst_ref=out_ref.at[:, p, q],
            send_sem=b_ssem.at[p],
            recv_sem=b_rsem.at[p],
            device_id=(chip * 2 + c, g),
            device_id_type=MESH,
        )

    def send_b(p):
        for dx, dy in OFFSETS:
            b_copy(p, dx, dy).start()
        out_ref[:, p, q] = z_recv[p, q]

    def b_all(p):
        return pltpu.make_async_remote_copy(
            src_ref=z_recv.at[p, pl.ds(0, CHIPS - 1)],
            dst_ref=z_recv.at[p, pl.ds(0, CHIPS - 1)],
            send_sem=b_ssem.at[p],
            recv_sem=b_rsem.at[p],
            device_id=(b, g),
            device_id_type=MESH,
        )

    for p in range(PHASES):
        combine(p)
        send_z(p)
        if p > 0:
            wait_z(p - 1)
            send_b(p - 1)
    wait_z(PHASES - 1)
    send_b(PHASES - 1)

    for p in range(PHASES):
        b_all(p).wait_recv()
    for p in range(PHASES):
        a_all(p).wait_send()
        for e in range(8):
            copy, here = z_copy(p, e)

            @pl.when(jnp.logical_not(here))
            def _():
                copy.wait_send()

        b_all(p).wait_send()


def on_device(band_coeffs, sign_table, slice_widths, owner_map):
    hbm = pl.BlockSpec(memory_space=pl.ANY)
    rows = pl.pallas_call(
        kernel,
        out_shape=jax.ShapeDtypeStruct((NZ, PHASES, CHIPS, 3, 1, 128), F32),
        in_specs=[hbm] * 4,
        out_specs=pl.BlockSpec(memory_space=pltpu.VMEM),
        scratch_shapes=[
            pltpu.VMEM((PHASES, BANDS, WIDE), F32),
            pltpu.VMEM((NPS, BANDS), jnp.int32),
            pltpu.VMEM((1, NSLICE), jnp.int32),
            pltpu.VMEM((1, NSLICE), jnp.int32),
            pltpu.VMEM((OUT, GROUPS * ROWS), BF16),
            pltpu.VMEM((OUT, 128), F32),
            pltpu.VMEM((PHASES, CHIPS, 2, ROWS, 128), F32),
            pltpu.VMEM((PHASES, GROUPS, ROWS, 128), F32),
            pltpu.VMEM((PHASES, 8, CHIPS, 3, 1, 128), F32),
            pltpu.VMEM((PHASES, CHIPS, NZ, 3, 1, 128), F32),
            pltpu.SemaphoreType.DMA((PHASES,)),
            pltpu.SemaphoreType.DMA((3,)),
            pltpu.SemaphoreType.DMA((PHASES,)),
            pltpu.SemaphoreType.DMA((PHASES,)),
            pltpu.SemaphoreType.DMA((PHASES, 8)),
            pltpu.SemaphoreType.DMA((PHASES, NZ)),
            pltpu.SemaphoreType.DMA((PHASES,)),
            pltpu.SemaphoreType.DMA((PHASES,)),
        ],
        compiler_params=pltpu.CompilerParams(
            collective_id=0, has_side_effects=True, vmem_limit_bytes=60 * 2**20
        ),
        name="pseudobands",
    )(band_coeffs, sign_table, slice_widths.reshape(1, NSLICE), owner_map.reshape(1, NSLICE))
    return jnp.transpose(rows[:, :, :, :, 0, :], (3, 0, 1, 2, 4)).reshape(3, NZ * SLAB)


def solution(mesh):
    return jax.shard_map(
        on_device,
        mesh=mesh,
        in_specs=(P("band", "gslab"), P(None, "band"), P(), P()),
        out_specs=P(("band", "gslab"), None),
        check_vma=False,
    )
```

time: 214 us -> 49.1 us (0.23)
  waiting for transfers between devices: 132 us -> 0 us
  Pallas kernels: 0 us -> 46.6 us
  matrix products: 35.5 us -> 0 us
  blocking collectives: 26.7 us -> 0 us
  between operations: 13.4 us -> 0.02 us
    reduce_scatter x1 -> x0, waiting for transfers between devices: 132 us -> none  [on_device(): lax.psum_scatter(jnp.dot(mixing, band_coeffs, precision=lax.Precision.HIG...]
    pallas_call x0 -> x1, Pallas kernels: none -> 46.6 us  [on_device(): pl.pallas_call(kernel, out_shape=jax.ShapeDtypeStruct((NZ, PHASES, CHIPS,...]
    dot_general x2 -> x0, matrix products: 35.5 us -> none  [the longest x1 34 us: on_device(): jnp.dot(mixing, band_coeffs, precision=lax.Precision.HIGHEST, preferred_e...]
    all_to_all x1 -> x0, blocking collectives: 26.7 us -> none  [on_device(): lax.all_to_all(summed, 'gslab', split_axis=0, concat_axis=1, tiled=True)]
  transfers between devices with their start and end apart: 1 -> 0, of which waited for: 1 -> 0; matrix products, arithmetic and copies ran while one was open for 0% -> 0% of each run, Pallas kernels for 0% -> 0%
where the time goes in v1:
time: 49.1 us; the launch traced here: 49 us
  Pallas kernels  46.6 us (95%)
  local copies, waits for them, and re-layouts  2.4 us (5%)
    pallas_call x1, Pallas kernels, on_device(): pl.pallas_call(kernel, out_shape=jax.ShapeDtypeStruct((NZ, PHASES, CHIPS,...  46.6 us
    unnamed x1, local copies, waits for them, and re-layouts  1.29 us
    transpose x1, local copies, waits for them, and re-layouts, on_device(): jnp.transpose(rows[:, :, :, :, 0, :], (3, 0, 1, 2, 4)).reshape(3, NZ * SLAB)  1.11 us

profile of v1, /device:TPU:1, one launch (start us, length us, event | category | flops | bytes accessed | tf_op | source)
XLA Modules:
  0.0 49.0 jit_solution(6479018487997879890)
XLA Ops:
  0.0 46.6 %pseudobands.1 = f32[8,3,16,3,1,128]{5,4,3,2,1,0:T(1,128)} custom-call(f32[384,6144]{1,0:T(8,128)} %band_ref.1, s32[12,384]{1,0:T(8,128)} %sign_ref.1, s32[1,64]{1,0:T(1,128)} %bitcast.11, s32[1,64]{1,0:T(1,128)} %bitcast.12), custom_call_target="tpu_custom_call" | custom-call | tf_op jit(solution)/shard_map/pseudobands/pallas_call | solution.py:293
  46.6 1.1 %copy.8 = f32[8,3,16,3,1,128]{5,2,1,0,3,4:T(8,128)S(1)} copy(f32[8,3,16,3,1,128]{5,4,3,2,1,0:T(1,128)} %pseudobands.1) | data formatting | bytes 1179648 | tf_op jit(solution)/shard_map/transpose | solution.py:323
  47.7 1.3 %copy.11 = f32[1,3,384,128]{3,1,2,0:T(4,128)} copy(f32[1,3,384,128]{3,2,1,0:T(8,128)S(1)} %bitcast.10) | data formatting | bytes 1179648

commit v2 on v1

v2 whole, which is shorter than its diff:
```python
import jax
import jax.numpy as jnp
from jax import lax
from jax.experimental import pallas as pl
from jax.experimental.pallas import tpu as pltpu
from jax.sharding import PartitionSpec as P

MESH = pl.DeviceIdType.MESH
F32 = jnp.float32
BF16 = jnp.bfloat16

NX, NY, NZ = 4, 4, 8
CHIPS = NX * NY
GROUPS = 2 * CHIPS
BANDS = 384
SLAB = 6144
PHASES = 3
WIDE = SLAB // PHASES
NPS = 12
TRI = 3
SLOTS = 5
ROWS = 16
NSLICE = 64
OUT = NSLICE * TRI
LAG = 2
VMEM_LIMIT = 52 * 10**6

OFFSETS = (
    (1, 0), (0, 1), (3, 0), (0, 3), (1, 1), (3, 3), (1, 3), (3, 1),
    (2, 0), (0, 2), (2, 1), (1, 2), (2, 3), (3, 2), (2, 2),
)


def iota(shape, dim):
    return lax.broadcasted_iota(jnp.int32, shape, dim)


def kernel(
    band_ref, sign_ref, width_ref, owner_ref, out_ref,
    coeffs, sign, width, owner, select, scale,
    a_send, a_recv, z_send, z_recv,
    load_sem, small_sem, a_ssem, a_rsem, z_ssem, z_rsem, b_ssem, b_rsem,
):
    b = lax.axis_index("band")
    g = lax.axis_index("gslab")
    c = lax.rem(b, 2)
    q = b // 2
    x = lax.rem(q, NX)
    y = q // NX
    parity = lax.rem(x + y, 2)

    def chip_at(dx, dy):
        return lax.rem(y + dy, NY) * NX + lax.rem(x + dx, NX)

    loads = [
        pltpu.make_async_copy(band_ref.at[:, pl.ds(p * WIDE, WIDE)], coeffs.at[p], load_sem.at[p])
        for p in range(PHASES)
    ]
    smalls = [
        pltpu.make_async_copy(src, dst, small_sem.at[i])
        for i, (src, dst) in enumerate(((sign_ref, sign), (width_ref, width), (owner_ref, owner)))
    ]
    for copy in smalls:
        copy.start()
    loads[0].start()

    barrier = pltpu.get_barrier_semaphore()
    greeted = 0
    for dc in range(2):
        for dx, dy in ((0, 0),) + OFFSETS:
            if (dc, dx, dy) != (0, 0, 0):
                peer = chip_at(dx, dy) * 2 + lax.rem(c + dc, 2)
                pl.semaphore_signal(barrier, inc=1, device_id=(peer, g), device_id_type=MESH)
                greeted += 1
        for dz in range(1, NZ):
            peer = q * 2 + lax.rem(c + dc, 2)
            pl.semaphore_signal(
                barrier, inc=1, device_id=(peer, lax.rem(g + dz, NZ)), device_id_type=MESH
            )
            greeted += 1
    for copy in loads[1:]:
        copy.start()

    for copy in smalls:
        copy.wait()
    width_row = width[...].astype(F32)
    owner_row = owner[...].astype(F32)
    ends = jnp.sum(
        jnp.where(iota((NSLICE, NSLICE), 1) <= iota((NSLICE, NSLICE), 0), width_row, 0.0),
        axis=1, keepdims=True,
    )
    first = b * BANDS
    band_row = (first + iota((1, BANDS), 1)).astype(F32)
    slice_row = jnp.sum(jnp.where(ends <= band_row, 1.0, 0.0), axis=0, keepdims=True)
    first_row = jnp.zeros((1, BANDS), F32) + first.astype(F32)
    first_slice = jnp.sum(jnp.where(ends <= first_row, 1.0, 0.0), axis=0, keepdims=True)
    row = iota((4 * ROWS, BANDS), 0)
    local = row & (ROWS - 1)
    slot = (local * 11) >> 5
    pseudo = (row >> 4) * TRI + local - slot * TRI
    sign_f = sign[...].astype(F32)
    signs = jnp.zeros((4 * ROWS, BANDS), F32)
    for j in range(NPS):
        signs = jnp.where(pseudo == j, sign_f[j : j + 1, :], signs)
    member = (slice_row - first_slice == slot.astype(F32)) & (local < SLOTS * TRI)
    mixing = jnp.where(member, signs, 0.0).astype(BF16)
    mixing = jnp.concatenate([mixing, mixing], axis=1)

    def partial_sums(p):
        loads[p].wait()

        @pl.loop(0, CHIPS // 2)
        def _(pair):
            part = coeffs[p, :, pl.ds(pl.multiple_of(pair * 256, 256), 256)]
            high = part.astype(BF16)
            low = (part - high.astype(F32)).astype(BF16)
            sums = jnp.dot(
                mixing, jnp.concatenate([high, low], axis=0), preferred_element_type=F32
            )
            for side in range(2):
                for part in range(4):
                    a_send[p, pair * 2 + side, part] = sums[
                        part * ROWS : (part + 1) * ROWS, side * 128 : (side + 1) * 128
                    ]

    def a_copy(p, s, dx, dy, dc):
        chip = chip_at(dx, dy)
        core = lax.rem(c + dc, 2)
        return pltpu.make_async_remote_copy(
            src_ref=a_send.at[p, chip, core * 2 + lax.rem(parity + (s + dx + dy), 2)],
            dst_ref=a_recv.at[p, s, b],
            send_sem=a_ssem.at[p, s],
            recv_sem=a_rsem.at[p, s],
            device_id=(chip * 2 + core, g),
            device_id_type=MESH,
        )

    def send_a(p):
        for s in range(2):
            for dx, dy in OFFSETS:
                for dc in range(2):
                    a_copy(p, s, dx, dy, dc).start()
            a_copy(p, s, 0, 0, 1).start()
            a_recv[p, s, b] = a_send[p, q, c * 2 + lax.rem(parity + s, 2)]

    def a_all(p, s):
        return pltpu.make_async_remote_copy(
            src_ref=a_recv.at[p, s, pl.ds(0, GROUPS - 1)],
            dst_ref=a_recv.at[p, s, pl.ds(0, GROUPS - 1)],
            send_sem=a_ssem.at[p, s],
            recv_sem=a_rsem.at[p, s],
            device_id=(b, g),
            device_id_type=MESH,
        )

    with jax.named_scope("sums#p=0"):
        partial_sums(0)
    with jax.named_scope("barrier"):
        pl.semaphore_wait(barrier, greeted)
    with jax.named_scope("send_a#p=0"):
        send_a(0)
    for p in range(1, PHASES):
        with jax.named_scope(f"sums#p={p}"):
            partial_sums(p)
        with jax.named_scope(f"send_a#p={p}"):
            send_a(p)

    source = iota((1, GROUPS * ROWS), 1)
    source_local = source & (ROWS - 1)
    source_slot = (source_local * 11) >> 5
    source_t = jnp.where(source_local < SLOTS * TRI, source_local - source_slot * TRI, -1)
    source_first = ((source >> 4) * BANDS).astype(F32)
    source_slice = (
        jnp.sum(jnp.where(ends <= source_first, 1.0, 0.0), axis=0, keepdims=True)
        + source_slot.astype(F32)
    )
    block = OUT // 4
    for e in range(4):
        in_slot, cc = e >> 1, e & 1
        r = iota((block, NSLICE), 0)
        place = (((r * 43) >> 7) * 2 + cc) * 2 + in_slot
        lane = iota((block, NSLICE), 1)
        target = jnp.sum(jnp.where(lane == place, owner_row, 0.0), axis=1, keepdims=True)
        bands = jnp.sum(
            jnp.where(lane.astype(F32) == target, width_row, 0.0), axis=1, keepdims=True
        )
        scale[e * block : (e + 1) * block, :] = jnp.broadcast_to(1.0 / jnp.sqrt(bands), (block, 128))
        r2 = iota((block, GROUPS * ROWS), 0)
        t2 = r2 - ((r2 * 43) >> 7) * TRI
        hit = (target == source_slice) & (t2 == source_t)
        select[e * block : (e + 1) * block, :] = jnp.where(hit, 1.0, 0.0).astype(BF16)

    in_class = lax.rem(g, 4) // 2 == c

    def combine(p, s):
        with jax.named_scope(f"wait_a#p={p}#s={s}"):
            a_all(p, s).wait_recv()
        part = a_recv[p, s].reshape(GROUPS * ROWS, 128)
        high = part.astype(BF16)
        low = (part - high.astype(F32)).astype(BF16)
        both = jnp.dot(
            select[...], jnp.concatenate([high, low], axis=1), preferred_element_type=F32
        )
        rows = (both[:, :128] + both[:, 128:]) * scale[...]
        for e in range(4):
            z_send[p, s, e] = rows[e * block : (e + 1) * block].reshape(CHIPS, TRI, 128)

    def z_copy(p, s, e):
        plane = (e >> 1) * 4 + 2 * c + lax.rem(parity + s, 2)
        core = e & 1
        copy = pltpu.make_async_remote_copy(
            src_ref=z_send.at[p, s, e],
            dst_ref=z_recv.at[p, :, g],
            send_sem=z_ssem.at[p, s, e],
            recv_sem=z_rsem.at[p, g],
            device_id=(q * 2 + core, plane),
            device_id_type=MESH,
        )
        here = (plane == g) & (core == c)
        return copy, here

    def send_z(p, s):
        for e in range(4):
            copy, here = z_copy(p, s, e)

            @pl.when(jnp.logical_not(here))
            def _():
                copy.start()

            @pl.when(here)
            def _():
                z_recv[p, :, g] = z_send[p, s, e]

    def wait_z(p):
        for plane in range(NZ):
            copy = pltpu.make_async_remote_copy(
                src_ref=z_send.at[p, 0, 0],
                dst_ref=z_recv.at[p, :, plane],
                send_sem=z_ssem.at[p, 0, 0],
                recv_sem=z_rsem.at[p, plane],
                device_id=(b, g),
                device_id_type=MESH,
            )

            @pl.when(jnp.logical_not(in_class & (g == plane)))
            def _():
                copy.wait_recv()

    def b_copy(p, dx, dy):
        chip = chip_at(dx, dy)
        return pltpu.make_async_remote_copy(
            src_ref=z_recv.at[p, chip],
            dst_ref=out_ref.at[:, p, q],
            send_sem=b_ssem.at[p],
            recv_sem=b_rsem.at[p],
            device_id=(chip * 2 + c, g),
            device_id_type=MESH,
        )

    def b_all(p):
        return pltpu.make_async_remote_copy(
            src_ref=z_recv.at[p, pl.ds(0, CHIPS - 1)],
            dst_ref=z_recv.at[p, pl.ds(0, CHIPS - 1)],
            send_sem=b_ssem.at[p],
            recv_sem=b_rsem.at[p],
            device_id=(b, g),
            device_id_type=MESH,
        )

    mine = lax.rem(g + parity, 2)

    def pass_on(p, s):
        @pl.when(mine == s)
        def _():
            with jax.named_scope(f"wait_z#p={p}#s={s}"):
                wait_z(p)
            for dx, dy in OFFSETS:
                b_copy(p, dx, dy).start()
            out_ref[:, p, q] = z_recv[p, q]

    steps = [(p, s) for p in range(PHASES) for s in range(2)]
    for k, step in enumerate(steps):
        combine(*step)
        with jax.named_scope(f"send_z#p={step[0]}#s={step[1]}"):
            send_z(*step)
        if k >= LAG:
            pass_on(*steps[k - LAG])
    for step in steps[-LAG:]:
        pass_on(*step)

    for p in range(PHASES):
        with jax.named_scope(f"wait_b#p={p}"):
            b_all(p).wait_recv()
    for p in range(PHASES):
        for s in range(2):
            a_all(p, s).wait_send()
            for e in range(4):
                copy, here = z_copy(p, s, e)

                @pl.when(jnp.logical_not(here))
                def _():
                    copy.wait_send()

        b_all(p).wait_send()


def on_device(band_coeffs, sign_table, slice_widths, owner_map):
    hbm = pl.BlockSpec(memory_space=pltpu.HBM)
    operands = (band_coeffs, sign_table, slice_widths.reshape(1, NSLICE), owner_map.reshape(1, NSLICE))
    operands = [pltpu.with_memory_space_constraint(v, pltpu.HBM) for v in operands]
    rows = pl.pallas_call(
        kernel,
        out_shape=jax.ShapeDtypeStruct((NZ, PHASES, CHIPS, TRI, 128), F32),
        in_specs=[hbm] * 4,
        out_specs=pl.BlockSpec(memory_space=pltpu.VMEM),
        scratch_shapes=[
            pltpu.VMEM((PHASES, BANDS, WIDE), F32),
            pltpu.VMEM((NPS, BANDS), jnp.int32),
            pltpu.VMEM((1, NSLICE), jnp.int32),
            pltpu.VMEM((1, NSLICE), jnp.int32),
            pltpu.VMEM((OUT, GROUPS * ROWS), BF16),
            pltpu.VMEM((OUT, 128), F32),
            pltpu.VMEM((PHASES, CHIPS, 4, ROWS, 128), F32),
            pltpu.VMEM((PHASES, 2, GROUPS, ROWS, 128), F32),
            pltpu.VMEM((PHASES, 2, 4, CHIPS, TRI, 128), F32),
            pltpu.VMEM((PHASES, CHIPS, NZ, TRI, 128), F32),
            pltpu.SemaphoreType.DMA((PHASES,)),
            pltpu.SemaphoreType.DMA((3,)),
            pltpu.SemaphoreType.DMA((PHASES, 2)),
            pltpu.SemaphoreType.DMA((PHASES, 2)),
            pltpu.SemaphoreType.DMA((PHASES, 2, 4)),
            pltpu.SemaphoreType.DMA((PHASES, NZ)),
            pltpu.SemaphoreType.DMA((PHASES,)),
            pltpu.SemaphoreType.DMA((PHASES,)),
        ],
        compiler_params=pltpu.CompilerParams(
            collective_id=0, has_side_effects=True, vmem_limit_bytes=VMEM_LIMIT
        ),
        name="pseudobands",
    )(*operands)
    return jnp.transpose(rows.reshape(-1, TRI, 128), (1, 0, 2)).reshape(TRI, NZ * SLAB)


def solution(mesh):
    return jax.shard_map(
        on_device,
        mesh=mesh,
        in_specs=(P("band", "gslab"), P(None, "band"), P(), P()),
        out_specs=P(("band", "gslab"), None),
        check_vma=False,
    )
```

time: 49.1 us -> 44.8 us (0.912)
  Pallas kernels: 46.6 us -> 43.9 us
  local copies, waits for them, and re-layouts: 2.4 us -> 0.88 us
    pallas_call x1, Pallas kernels: 46.6 us -> 43.9 us  [on_device(): pl.pallas_call(kernel, out_shape=jax.ShapeDtypeStruct((NZ, PHASES, CHIPS,...]
    transpose x1 -> x0, local copies, waits for them, and re-layouts: 1.11 us -> none  [on_device(): jnp.transpose(rows[:, :, :, :, 0, :], (3, 0, 1, 2, 4)).reshape(3, NZ * SLAB)]
where the time goes in v2:
time: 44.8 us
  Pallas kernels  43.9 us (98%)
  local copies, waits for them, and re-layouts  0.88 us (2%)
    pallas_call x1, Pallas kernels, on_device(): pl.pallas_call(kernel, out_shape=jax.ShapeDtypeStruct((NZ, PHASES, CHIPS,...  43.9 us

profile of v2, /device:TPU:1, one launch (start us, length us, event | category | flops | bytes accessed | tf_op | source)
XLA Modules:
  0.0 44.8 jit_solution(14934986113162390180)
XLA Ops:
  0.0 43.9 %pseudobands.1 = f32[8,3,16,3,128]{4,3,2,1,0:T(4,128)S(1)} custom-call(f32[384,6144]{1,0:T(8,128)} %band_ref.1, s32[12,384]{1,0:T(8,128)} %sign_ref.1, s32[1,64]{1,0:T(1,128)} %bitcast.8, s32[1,64]{1,0:T(1,128)} %bitcast.9), custom_call_target="tpu_custom_call" | custom-call | tf_op jit(solution)/shard_map/pseudobands/pallas_call | solution.py:311
  43.9 0.9 %copy.7 = f32[3,49152]{1,0:T(4,128)} copy(f32[3,49152]{1,0:T(4,128)S(1)} %bitcast.7) | data formatting | bytes 1179648

commit v3 on v2

--- a/solution.py
+++ b/solution.py
@@ -20,15 +20,19 @@
 TRI = 3
 SLOTS = 5
 ROWS = 16
+USED = SLOTS * TRI
 NSLICE = 64
 OUT = NSLICE * TRI
 LAG = 2
+DIRECT = ((2, 0), (2, 1))
 VMEM_LIMIT = 52 * 10**6
 
 OFFSETS = (
     (1, 0), (0, 1), (3, 0), (0, 3), (1, 1), (3, 3), (1, 3), (3, 1),
     (2, 0), (0, 2), (2, 1), (1, 2), (2, 3), (3, 2), (2, 2),
 )
+
+A_ORDER = ((2, 2), (2, 1), (2, 3), (2, 0), (1, 2), (3, 2), (1, 1), (3, 3), (1, 3), (3, 1), (1, 0), (3, 0), (0, 2), (0, 1), (0, 3))
 
 
 def iota(shape, dim):
@@ -66,18 +70,20 @@
 
     barrier = pltpu.get_barrier_semaphore()
     greeted = 0
-    for dc in range(2):
-        for dx, dy in ((0, 0),) + OFFSETS:
-            if (dc, dx, dy) != (0, 0, 0):
-                peer = chip_at(dx, dy) * 2 + lax.rem(c + dc, 2)
-                pl.semaphore_signal(barrier, inc=1, device_id=(peer, g), device_id_type=MESH)
-                greeted += 1
-        for dz in range(1, NZ):
-            peer = q * 2 + lax.rem(c + dc, 2)
+    for dz in (4, 3, 5, 2, 6, 1, 7):
+        for core in range(2):
             pl.semaphore_signal(
-                barrier, inc=1, device_id=(peer, lax.rem(g + dz, NZ)), device_id_type=MESH
+                barrier, inc=1, device_id=(q * 2 + core, lax.rem(g + dz, NZ)), device_id_type=MESH
             )
             greeted += 1
+    for dx, dy in reversed(OFFSETS):
+        for core in range(2):
+            pl.semaphore_signal(
+                barrier, inc=1, device_id=(chip_at(dx, dy) * 2 + core, g), device_id_type=MESH
+            )
+            greeted += 1
+    pl.semaphore_signal(barrier, inc=1, device_id=(q * 2 + 1 - c, g), device_id_type=MESH)
+    greeted += 1
     for copy in loads[1:]:
         copy.start()
 
@@ -120,7 +126,7 @@
             for side in range(2):
                 for part in range(4):
                     a_send[p, pair * 2 + side, part] = sums[
-                        part * ROWS : (part + 1) * ROWS, side * 128 : (side + 1) * 128
+                        part * ROWS : part * ROWS + USED, side * 128 : (side + 1) * 128
                     ]
 
     def a_copy(p, s, dx, dy, dc):
@@ -137,7 +143,7 @@
 
     def send_a(p):
         for s in range(2):
-            for dx, dy in OFFSETS:
+            for dx, dy in A_ORDER:
                 for dc in range(2):
                     a_copy(p, s, dx, dy, dc).start()
             a_copy(p, s, 0, 0, 1).start()
@@ -192,10 +198,14 @@
 
     in_class = lax.rem(g, 4) // 2 == c
 
+    def z_rows(s, e):
+        return pl.ds((s * 4 + e) * CHIPS, CHIPS)
+
     def combine(p, s):
         with jax.named_scope(f"wait_a#p={p}#s={s}"):
             a_all(p, s).wait_recv()
-        part = a_recv[p, s].reshape(GROUPS * ROWS, 128)
+        part = jnp.concatenate([a_recv[p, s], jnp.zeros((GROUPS, ROWS - USED, 128), F32)], axis=1)
+        part = part.reshape(GROUPS * ROWS, 128)
         high = part.astype(BF16)
         low = (part - high.astype(F32)).astype(BF16)
         both = jnp.dot(
@@ -203,13 +213,13 @@
         )
         rows = (both[:, :128] + both[:, 128:]) * scale[...]
         for e in range(4):
-            z_send[p, s, e] = rows[e * block : (e + 1) * block].reshape(CHIPS, TRI, 128)
+            z_send[p, z_rows(s, e)] = rows[e * block : (e + 1) * block].reshape(CHIPS, TRI, 128)
 
     def z_copy(p, s, e):
         plane = (e >> 1) * 4 + 2 * c + lax.rem(parity + s, 2)
         core = e & 1
         copy = pltpu.make_async_remote_copy(
-            src_ref=z_send.at[p, s, e],
+            src_ref=z_send.at[p, z_rows(s, e)],
             dst_ref=z_recv.at[p, :, g],
             send_sem=z_ssem.at[p, s, e],
             recv_sem=z_rsem.at[p, g],
@@ -229,12 +239,12 @@
 
             @pl.when(here)
             def _():
-                z_recv[p, :, g] = z_send[p, s, e]
+                z_recv[p, :, g] = z_send[p, z_rows(s, e)]
 
     def wait_z(p):
         for plane in range(NZ):
             copy = pltpu.make_async_remote_copy(
-                src_ref=z_send.at[p, 0, 0],
+                src_ref=z_send.at[p, z_rows(0, 0)],
                 dst_ref=z_recv.at[p, :, plane],
                 send_sem=z_ssem.at[p, 0, 0],
                 recv_sem=z_rsem.at[p, plane],
@@ -267,6 +277,45 @@
             device_id_type=MESH,
         )
 
+    def d_copy(p, s, e, dx, dy):
+        plane = (e >> 1) * 4 + 2 * c + lax.rem(parity + s, 2)
+        core = e & 1
+        chip = chip_at(dx, dy)
+        copy = pltpu.make_async_remote_copy(
+            src_ref=z_send.at[p, (s * 4 + e) * CHIPS + chip],
+            dst_ref=out_ref.at[g, p, q],
+            send_sem=z_ssem.at[p, s, 0],
+            recv_sem=b_rsem.at[p],
+            device_id=(chip * 2 + core, plane),
+            device_id_type=MESH,
+        )
+        return copy, (plane == g) & (core == c)
+
+    def send_d(p, s):
+        for dx, dy in tuple(reversed(OFFSETS)):
+            for e in range(4):
+                d_copy(p, s, e, dx, dy)[0].start()
+        for e in range(4):
+            copy, here = d_copy(p, s, e, 0, 0)
+
+            @pl.when(jnp.logical_not(here))
+            def _():
+                copy.start()
+
+            @pl.when(here)
+            def _():
+                out_ref[g, p, q] = z_send[p, (s * 4 + e) * CHIPS + q]
+
+    def d_all(p, s, count):
+        return pltpu.make_async_remote_copy(
+            src_ref=z_send.at[p, pl.ds(0, count)],
+            dst_ref=z_send.at[p, pl.ds(0, count)],
+            send_sem=z_ssem.at[p, s, 0],
+            recv_sem=b_rsem.at[p],
+            device_id=(b, g),
+            device_id_type=MESH,
+        )
+
     mine = lax.rem(g + parity, 2)
 
     def pass_on(p, s):
@@ -274,7 +323,7 @@
         def _():
             with jax.named_scope(f"wait_z#p={p}#s={s}"):
                 wait_z(p)
-            for dx, dy in OFFSETS:
+            for dx, dy in reversed(OFFSETS):
                 b_copy(p, dx, dy).start()
             out_ref[:, p, q] = z_recv[p, q]
 
@@ -282,26 +331,54 @@
     for k, step in enumerate(steps):
         combine(*step)
         with jax.named_scope(f"send_z#p={step[0]}#s={step[1]}"):
-            send_z(*step)
-        if k >= LAG:
+            (send_d if step in DIRECT else send_z)(*step)
+        if k >= LAG and steps[k - LAG] not in DIRECT:
             pass_on(*steps[k - LAG])
     for step in steps[-LAG:]:
-        pass_on(*step)
-
-    for p in range(PHASES):
-        with jax.named_scope(f"wait_b#p={p}"):
-            b_all(p).wait_recv()
+        if step not in DIRECT:
+            pass_on(*step)
+
     for p in range(PHASES):
         for s in range(2):
             a_all(p, s).wait_send()
-            for e in range(4):
-                copy, here = z_copy(p, s, e)
-
-                @pl.when(jnp.logical_not(here))
+            if (p, s) in DIRECT:
+                own = in_class & (mine == s)
+
+                @pl.when(own)
                 def _():
-                    copy.wait_send()
-
-        b_all(p).wait_send()
+                    d_all(p, s, 4 * CHIPS - 1).wait_send()
+
+                @pl.when(jnp.logical_not(own))
+                def _():
+                    d_all(p, s, 4 * CHIPS).wait_send()
+
+            else:
+                for e in range(4):
+                    copy, here = z_copy(p, s, e)
+
+                    @pl.when(jnp.logical_not(here))
+                    def _():
+                        copy.wait_send()
+
+    for p in range(PHASES):
+        for s in range(2):
+
+            @pl.when(mine == s)
+            def _():
+                with jax.named_scope(f"wait_b#p={p}#s={s}"):
+                    if (p, s) in DIRECT:
+
+                        @pl.when(in_class)
+                        def _():
+                            d_all(p, s, NZ * CHIPS - 1).wait_recv()
+
+                        @pl.when(jnp.logical_not(in_class))
+                        def _():
+                            d_all(p, s, NZ * CHIPS).wait_recv()
+
+                    else:
+                        b_all(p).wait_recv()
+                        b_all(p).wait_send()
 
 
 def on_device(band_coeffs, sign_table, slice_widths, owner_map):
@@ -320,9 +397,9 @@
             pltpu.VMEM((1, NSLICE), jnp.int32),
             pltpu.VMEM((OUT, GROUPS * ROWS), BF16),
             pltpu.VMEM((OUT, 128), F32),
-            pltpu.VMEM((PHASES, CHIPS, 4, ROWS, 128), F32),
-            pltpu.VMEM((PHASES, 2, GROUPS, ROWS, 128), F32),
-            pltpu.VMEM((PHASES, 2, 4, CHIPS, TRI, 128), F32),
+            pltpu.VMEM((PHASES, CHIPS, 4, USED, 128), F32),
+            pltpu.VMEM((PHASES, 2, GROUPS, USED, 128), F32),
+            pltpu.VMEM((PHASES, 2 * 4 * CHIPS, TRI, 128), F32),
             pltpu.VMEM((PHASES, CHIPS, NZ, TRI, 128), F32),
             pltpu.SemaphoreType.DMA((PHASES,)),
             pltpu.SemaphoreType.DMA((3,)),

time: 44.8 us -> 40.5 us (0.904)
  Pallas kernels: 43.9 us -> 39.5 us
    pallas_call x1, Pallas kernels: 43.9 us -> 39.5 us  [on_device(): pl.pallas_call(kernel, out_shape=jax.ShapeDtypeStruct((NZ, PHASES, CHIPS,...]
where the time goes in v3:
time: 40.5 us; the launch traced here: 40.4 us
  Pallas kernels  39.5 us (98%)
  local copies, waits for them, and re-layouts  0.88 us (2%)
    pallas_call x1, Pallas kernels, on_device(): pl.pallas_call(kernel, out_shape=jax.ShapeDtypeStruct((NZ, PHASES, CHIPS,...  39.5 us
    unnamed x1, local copies, waits for them, and re-layouts  0.88 us

profile of v3, /device:TPU:1, one launch (start us, length us, event | category | flops | bytes accessed | tf_op | source)
XLA Modules:
  0.0 40.4 jit_solution(9183323737532580179)
XLA Ops:
  0.0 39.5 %pseudobands.1 = f32[8,3,16,3,128]{4,3,2,1,0:T(4,128)S(1)} custom-call(f32[384,6144]{1,0:T(8,128)} %band_ref.1, s32[12,384]{1,0:T(8,128)} %sign_ref.1, s32[1,64]{1,0:T(1,128)} %bitcast.8, s32[1,64]{1,0:T(1,128)} %bitcast.9), custom_call_target="tpu_custom_call" | custom-call | tf_op jit(solution)/shard_map/pseudobands/pallas_call | solution.py:388
  39.5 0.9 %copy.7 = f32[3,49152]{1,0:T(4,128)} copy(f32[3,49152]{1,0:T(4,128)S(1)} %bitcast.7) | data formatting | bytes 1179648

commit v4 on v3

--- a/solution.py
+++ b/solution.py
@@ -21,6 +21,9 @@
 SLOTS = 5
 ROWS = 16
 USED = SLOTS * TRI
+CHIP_SLOTS = 9
+CHIP_ROWS = 32
+CHIP_USED = CHIP_SLOTS * TRI
 NSLICE = 64
 OUT = NSLICE * TRI
 LAG = 2
@@ -41,9 +44,9 @@
 
 def kernel(
     band_ref, sign_ref, width_ref, owner_ref, out_ref,
-    coeffs, sign, width, owner, select, scale,
-    a_send, a_recv, z_send, z_recv,
-    load_sem, small_sem, a_ssem, a_rsem, z_ssem, z_rsem, b_ssem, b_rsem,
+    coeffs, sign, width, owner, select, chip_select, scale,
+    a_send, a_recv, d_send, d_recv, m_send, m_recv, z_send, z_recv,
+    load_sem, small_sem, a_ssem, a_rsem, d_ssem, d_rsem, z_ssem, b_ssem, b_rsem,
 ):
     b = lax.axis_index("band")
     g = lax.axis_index("gslab")
@@ -112,10 +115,25 @@
     mixing = jnp.where(member, signs, 0.0).astype(BF16)
     mixing = jnp.concatenate([mixing, mixing], axis=1)
 
-    def partial_sums(p):
+    def chip_mixing():
+        row = iota((4 * CHIP_ROWS, BANDS), 0)
+        local = row & (CHIP_ROWS - 1)
+        slot = (local * 11) >> 5
+        half = jnp.where(row < 2 * CHIP_ROWS, c, 1 - c)
+        pseudo = (half * 2 + ((row >> 5) & 1)) * TRI + local - slot * TRI
+        signs = jnp.zeros((4 * CHIP_ROWS, BANDS), F32)
+        for j in range(NPS):
+            signs = jnp.where(pseudo == j, sign_f[j : j + 1, :], signs)
+        chip_row = jnp.zeros((1, BANDS), F32) + (q * (2 * BANDS)).astype(F32)
+        chip_slice = jnp.sum(jnp.where(ends <= chip_row, 1.0, 0.0), axis=0, keepdims=True)
+        member = (slice_row - chip_slice == slot.astype(F32)) & (local < CHIP_USED)
+        mixing = jnp.where(member, signs, 0.0).astype(BF16)
+        return jnp.concatenate([mixing, mixing], axis=1)
+
+    def partial_sums(p, mixing, store):
         loads[p].wait()
 
-        @pl.loop(0, CHIPS // 2)
+        @pl.loop(0, CHIPS // 2, unroll=4)
         def _(pair):
             part = coeffs[p, :, pl.ds(pl.multiple_of(pair * 256, 256), 256)]
             high = part.astype(BF16)
@@ -124,35 +142,79 @@
                 mixing, jnp.concatenate([high, low], axis=0), preferred_element_type=F32
             )
             for side in range(2):
-                for part in range(4):
-                    a_send[p, pair * 2 + side, part] = sums[
-                        part * ROWS : part * ROWS + USED, side * 128 : (side + 1) * 128
-                    ]
-
-    def a_copy(p, s, dx, dy, dc):
+                store(pair * 2 + side, sums[:, side * 128 : (side + 1) * 128])
+
+    def store_groups(chip, sums):
+        for part in range(4):
+            a_send[chip, part] = sums[part * ROWS : part * ROWS + USED]
+
+    def store_chips(p):
+        def store(chip, sums):
+            for h in range(2):
+                own = h * CHIP_ROWS
+                m_send[p - 1, chip, h] = sums[own : own + CHIP_USED]
+                other = own + 2 * CHIP_ROWS
+                d_send[p - 1, chip, h] = sums[other : other + CHIP_USED]
+
+        return store
+
+    def a_copy(s, dx, dy, dc):
         chip = chip_at(dx, dy)
         core = lax.rem(c + dc, 2)
         return pltpu.make_async_remote_copy(
-            src_ref=a_send.at[p, chip, core * 2 + lax.rem(parity + (s + dx + dy), 2)],
-            dst_ref=a_recv.at[p, s, b],
-            send_sem=a_ssem.at[p, s],
-            recv_sem=a_rsem.at[p, s],
+            src_ref=a_send.at[chip, core * 2 + lax.rem(parity + (s + dx + dy), 2)],
+            dst_ref=a_recv.at[s, b],
+            send_sem=a_ssem.at[0, s],
+            recv_sem=a_rsem.at[0, s],
             device_id=(chip * 2 + core, g),
             device_id_type=MESH,
         )
 
-    def send_a(p):
+    def send_a():
         for s in range(2):
             for dx, dy in A_ORDER:
                 for dc in range(2):
-                    a_copy(p, s, dx, dy, dc).start()
-            a_copy(p, s, 0, 0, 1).start()
-            a_recv[p, s, b] = a_send[p, q, c * 2 + lax.rem(parity + s, 2)]
+                    a_copy(s, dx, dy, dc).start()
+            a_copy(s, 0, 0, 1).start()
+            a_recv[s, b] = a_send[q, c * 2 + lax.rem(parity + s, 2)]
+
+    def swap(p):
+        return pltpu.make_async_remote_copy(
+            src_ref=d_send.at[p - 1],
+            dst_ref=d_recv.at[p - 1],
+            send_sem=d_ssem.at[p - 1],
+            recv_sem=d_rsem.at[p - 1],
+            device_id=(q * 2 + 1 - c, g),
+            device_id_type=MESH,
+        )
+
+    def m_copy(p, s, dx, dy):
+        chip = chip_at(dx, dy)
+        return pltpu.make_async_remote_copy(
+            src_ref=m_send.at[p - 1, chip, lax.rem(parity + (s + dx + dy), 2)],
+            dst_ref=m_recv.at[p - 1, s, q],
+            send_sem=a_ssem.at[p, s],
+            recv_sem=a_rsem.at[p, s],
+            device_id=(chip * 2 + c, g),
+            device_id_type=MESH,
+        )
+
+    def send_m(p):
+        swap(p).wait_recv()
+        m_send[p - 1] = m_send[p - 1] + d_recv[p - 1]
+        for s in range(2):
+            for dx, dy in A_ORDER:
+                m_copy(p, s, dx, dy).start()
+            m_recv[p - 1, s, q] = m_send[p - 1, q, lax.rem(parity + s, 2)]
 
     def a_all(p, s):
-        return pltpu.make_async_remote_copy(
-            src_ref=a_recv.at[p, s, pl.ds(0, GROUPS - 1)],
-            dst_ref=a_recv.at[p, s, pl.ds(0, GROUPS - 1)],
+        if p == 0:
+            ref = a_recv.at[s, pl.ds(0, GROUPS - 1)]
+        else:
+            ref = m_recv.at[p - 1, s, pl.ds(0, CHIPS - 1)]
+        return pltpu.make_async_remote_copy(
+            src_ref=ref,
+            dst_ref=ref,
             send_sem=a_ssem.at[p, s],
             recv_sem=a_rsem.at[p, s],
             device_id=(b, g),
@@ -160,25 +222,32 @@
         )
 
     with jax.named_scope("sums#p=0"):
-        partial_sums(0)
+        partial_sums(0, mixing, store_groups)
     with jax.named_scope("barrier"):
         pl.semaphore_wait(barrier, greeted)
     with jax.named_scope("send_a#p=0"):
-        send_a(0)
+        send_a()
+    mixing = chip_mixing()
     for p in range(1, PHASES):
         with jax.named_scope(f"sums#p={p}"):
-            partial_sums(p)
-        with jax.named_scope(f"send_a#p={p}"):
-            send_a(p)
-
-    source = iota((1, GROUPS * ROWS), 1)
-    source_local = source & (ROWS - 1)
-    source_slot = (source_local * 11) >> 5
-    source_t = jnp.where(source_local < SLOTS * TRI, source_local - source_slot * TRI, -1)
-    source_first = ((source >> 4) * BANDS).astype(F32)
-    source_slice = (
-        jnp.sum(jnp.where(ends <= source_first, 1.0, 0.0), axis=0, keepdims=True)
-        + source_slot.astype(F32)
+            partial_sums(p, mixing, store_chips(p))
+        swap(p).start()
+    for p in range(1, PHASES):
+        with jax.named_scope(f"send_m#p={p}"):
+            send_m(p)
+
+    def source_rows(per_source, used, bands):
+        source = iota((1, GROUPS * ROWS), 1)
+        local = source & (per_source - 1)
+        slot = (local * 11) >> 5
+        t = jnp.where(local < used, local - slot * TRI, -1)
+        first = ((source // per_source) * bands).astype(F32)
+        begun = jnp.sum(jnp.where(ends <= first, 1.0, 0.0), axis=0, keepdims=True)
+        return begun + slot.astype(F32), t
+
+    sources = (
+        (select, source_rows(ROWS, USED, BANDS)),
+        (chip_select, source_rows(CHIP_ROWS, CHIP_USED, 2 * BANDS)),
     )
     block = OUT // 4
     for e in range(4):
@@ -193,8 +262,9 @@
         scale[e * block : (e + 1) * block, :] = jnp.broadcast_to(1.0 / jnp.sqrt(bands), (block, 128))
         r2 = iota((block, GROUPS * ROWS), 0)
         t2 = r2 - ((r2 * 43) >> 7) * TRI
-        hit = (target == source_slice) & (t2 == source_t)
-        select[e * block : (e + 1) * block, :] = jnp.where(hit, 1.0, 0.0).astype(BF16)
+        for matrix, (source_slice, source_t) in sources:
+            hit = (target == source_slice) & (t2 == source_t)
+            matrix[e * block : (e + 1) * block, :] = jnp.where(hit, 1.0, 0.0).astype(BF16)
 
     in_class = lax.rem(g, 4) // 2 == c
 
@@ -204,12 +274,15 @@
     def combine(p, s):
         with jax.named_scope(f"wait_a#p={p}#s={s}"):
             a_all(p, s).wait_recv()
-        part = jnp.concatenate([a_recv[p, s], jnp.zeros((GROUPS, ROWS - USED, 128), F32)], axis=1)
-        part = part.reshape(GROUPS * ROWS, 128)
+        if p == 0:
+            matrix, part, spare = select, a_recv[s], (GROUPS, ROWS - USED, 128)
+        else:
+            matrix, part, spare = chip_select, m_recv[p - 1, s], (CHIPS, CHIP_ROWS - CHIP_USED, 128)
+        part = jnp.concatenate([part, jnp.zeros(spare, F32)], axis=1).reshape(GROUPS * ROWS, 128)
         high = part.astype(BF16)
         low = (part - high.astype(F32)).astype(BF16)
         both = jnp.dot(
-            select[...], jnp.concatenate([high, low], axis=1), preferred_element_type=F32
+            matrix[...], jnp.concatenate([high, low], axis=1), preferred_element_type=F32
         )
         rows = (both[:, :128] + both[:, 128:]) * scale[...]
         for e in range(4):
@@ -221,8 +294,8 @@
         copy = pltpu.make_async_remote_copy(
             src_ref=z_send.at[p, z_rows(s, e)],
             dst_ref=z_recv.at[p, :, g],
-            send_sem=z_ssem.at[p, s, e],
-            recv_sem=z_rsem.at[p, g],
+            send_sem=z_ssem.at[p, s],
+            recv_sem=b_rsem.at[PHASES + p],
             device_id=(q * 2 + core, plane),
             device_id_type=MESH,
         )
@@ -241,20 +314,24 @@
             def _():
                 z_recv[p, :, g] = z_send[p, z_rows(s, e)]
 
+    def blocks(p, s, count):
+        return pltpu.make_async_remote_copy(
+            src_ref=z_send.at[p, pl.ds(0, count)],
+            dst_ref=z_send.at[p, pl.ds(0, count)],
+            send_sem=z_ssem.at[p, s],
+            recv_sem=b_rsem.at[PHASES + p],
+            device_id=(b, g),
+            device_id_type=MESH,
+        )
+
     def wait_z(p):
-        for plane in range(NZ):
-            copy = pltpu.make_async_remote_copy(
-                src_ref=z_send.at[p, z_rows(0, 0)],
-                dst_ref=z_recv.at[p, :, plane],
-                send_sem=z_ssem.at[p, 0, 0],
-                recv_sem=z_rsem.at[p, plane],
-                device_id=(b, g),
-                device_id_type=MESH,
-            )
-
-            @pl.when(jnp.logical_not(in_class & (g == plane)))
-            def _():
-                copy.wait_recv()
+        @pl.when(in_class)
+        def _():
+            blocks(p, 0, (NZ - 1) * CHIPS).wait_recv()
+
+        @pl.when(jnp.logical_not(in_class))
+        def _():
+            blocks(p, 0, NZ * CHIPS).wait_recv()
 
     def b_copy(p, dx, dy):
         chip = chip_at(dx, dy)
@@ -284,7 +361,7 @@
         copy = pltpu.make_async_remote_copy(
             src_ref=z_send.at[p, (s * 4 + e) * CHIPS + chip],
             dst_ref=out_ref.at[g, p, q],
-            send_sem=z_ssem.at[p, s, 0],
+            send_sem=z_ssem.at[p, s],
             recv_sem=b_rsem.at[p],
             device_id=(chip * 2 + core, plane),
             device_id_type=MESH,
@@ -310,7 +387,7 @@
         return pltpu.make_async_remote_copy(
             src_ref=z_send.at[p, pl.ds(0, count)],
             dst_ref=z_send.at[p, pl.ds(0, count)],
-            send_sem=z_ssem.at[p, s, 0],
+            send_sem=z_ssem.at[p, s],
             recv_sem=b_rsem.at[p],
             device_id=(b, g),
             device_id_type=MESH,
@@ -341,24 +418,19 @@
     for p in range(PHASES):
         for s in range(2):
             a_all(p, s).wait_send()
-            if (p, s) in DIRECT:
-                own = in_class & (mine == s)
-
-                @pl.when(own)
-                def _():
-                    d_all(p, s, 4 * CHIPS - 1).wait_send()
-
-                @pl.when(jnp.logical_not(own))
-                def _():
-                    d_all(p, s, 4 * CHIPS).wait_send()
-
-            else:
-                for e in range(4):
-                    copy, here = z_copy(p, s, e)
-
-                    @pl.when(jnp.logical_not(here))
-                    def _():
-                        copy.wait_send()
+            own = in_class & (mine == s)
+            part = 1 if (p, s) in DIRECT else CHIPS
+
+            @pl.when(own)
+            def _():
+                blocks(p, s, 4 * CHIPS - part).wait_send()
+
+            @pl.when(jnp.logical_not(own))
+            def _():
+                blocks(p, s, 4 * CHIPS).wait_send()
+
+    for p in range(1, PHASES):
+        swap(p).wait_send()
 
     for p in range(PHASES):
         for s in range(2):
@@ -396,19 +468,25 @@
             pltpu.VMEM((1, NSLICE), jnp.int32),
             pltpu.VMEM((1, NSLICE), jnp.int32),
             pltpu.VMEM((OUT, GROUPS * ROWS), BF16),
+            pltpu.VMEM((OUT, GROUPS * ROWS), BF16),
             pltpu.VMEM((OUT, 128), F32),
-            pltpu.VMEM((PHASES, CHIPS, 4, USED, 128), F32),
-            pltpu.VMEM((PHASES, 2, GROUPS, USED, 128), F32),
+            pltpu.VMEM((CHIPS, 4, USED, 128), F32),
+            pltpu.VMEM((2, GROUPS, USED, 128), F32),
+            pltpu.VMEM((PHASES - 1, CHIPS, 2, CHIP_USED, 128), F32),
+            pltpu.VMEM((PHASES - 1, CHIPS, 2, CHIP_USED, 128), F32),
+            pltpu.VMEM((PHASES - 1, CHIPS, 2, CHIP_USED, 128), F32),
+            pltpu.VMEM((PHASES - 1, 2, CHIPS, CHIP_USED, 128), F32),
             pltpu.VMEM((PHASES, 2 * 4 * CHIPS, TRI, 128), F32),
             pltpu.VMEM((PHASES, CHIPS, NZ, TRI, 128), F32),
             pltpu.SemaphoreType.DMA((PHASES,)),
             pltpu.SemaphoreType.DMA((3,)),
             pltpu.SemaphoreType.DMA((PHASES, 2)),
             pltpu.SemaphoreType.DMA((PHASES, 2)),
-            pltpu.SemaphoreType.DMA((PHASES, 2, 4)),
-            pltpu.SemaphoreType.DMA((PHASES, NZ)),
+            pltpu.SemaphoreType.DMA((PHASES - 1,)),
+            pltpu.SemaphoreType.DMA((PHASES - 1,)),
+            pltpu.SemaphoreType.DMA((PHASES, 2)),
             pltpu.SemaphoreType.DMA((PHASES,)),
-            pltpu.SemaphoreType.DMA((PHASES,)),
+            pltpu.SemaphoreType.DMA((2 * PHASES,)),
         ],
         compiler_params=pltpu.CompilerParams(
             collective_id=0, has_side_effects=True, vmem_limit_bytes=VMEM_LIMIT

time: 40.5 us -> 38.8 us (0.958)
  Pallas kernels: 39.5 us -> 37.9 us
    pallas_call x1, Pallas kernels: 39.5 us -> 37.9 us  [on_device(): pl.pallas_call(kernel, out_shape=jax.ShapeDtypeStruct((NZ, PHASES, CHIPS,...]
where the time goes in v4:
time: 38.8 us; the launch traced here: 38.7 us
  Pallas kernels  37.9 us (98%)
  local copies, waits for them, and re-layouts  0.88 us (2%)
    pallas_call x1, Pallas kernels, on_device(): pl.pallas_call(kernel, out_shape=jax.ShapeDtypeStruct((NZ, PHASES, CHIPS,...  37.9 us
    unnamed x1, local copies, waits for them, and re-layouts  0.88 us

profile of v4, /device:TPU:1, one launch (start us, length us, event | category | flops | bytes accessed | tf_op | source)
XLA Modules:
  0.0 38.7 jit_solution(6676202669068469811)
XLA Ops:
  0.0 37.9 %pseudobands.1 = f32[8,3,16,3,128]{4,3,2,1,0:T(4,128)S(1)} custom-call(f32[384,6144]{1,0:T(8,128)} %band_ref.1, s32[12,384]{1,0:T(8,128)} %sign_ref.1, s32[1,64]{1,0:T(1,128)} %bitcast.8, s32[1,64]{1,0:T(1,128)} %bitcast.9), custom_call_target="tpu_custom_call" | custom-call | tf_op jit(solution)/shard_map/pseudobands/pallas_call | solution.py:460
  37.9 0.9 %copy.7 = f32[3,49152]{1,0:T(4,128)} copy(f32[3,49152]{1,0:T(4,128)S(1)} %bitcast.7) | data formatting | bytes 1179648

commit v5 on v4

--- a/solution.py
+++ b/solution.py
@@ -27,7 +27,6 @@
 NSLICE = 64
 OUT = NSLICE * TRI
 LAG = 2
-DIRECT = ((2, 0), (2, 1))
 VMEM_LIMIT = 52 * 10**6
 
 OFFSETS = (
@@ -56,6 +55,12 @@
     y = q // NX
     parity = lax.rem(x + y, 2)
 
+    ring = lax.rem(g - 2 * c + NZ, 4)
+    last = 1 - lax.rem((ring + 1) // 2, 2)
+
+    def triple(p, s, shift=0):
+        return lax.rem(last + 1 + s, 2) if p == PHASES - 1 else lax.rem(parity + (s + shift), 2)
+
     def chip_at(dx, dy):
         return lax.rem(y + dy, NY) * NX + lax.rem(x + dx, NX)
 
@@ -73,12 +78,6 @@
 
     barrier = pltpu.get_barrier_semaphore()
     greeted = 0
-    for dz in (4, 3, 5, 2, 6, 1, 7):
-        for core in range(2):
-            pl.semaphore_signal(
-                barrier, inc=1, device_id=(q * 2 + core, lax.rem(g + dz, NZ)), device_id_type=MESH
-            )
-            greeted += 1
     for dx, dy in reversed(OFFSETS):
         for core in range(2):
             pl.semaphore_signal(
@@ -87,6 +86,12 @@
             greeted += 1
     pl.semaphore_signal(barrier, inc=1, device_id=(q * 2 + 1 - c, g), device_id_type=MESH)
     greeted += 1
+    for dz in (4, 3, 5, 2, 6, 1, 7):
+        for core in range(2):
+            pl.semaphore_signal(
+                barrier, inc=1, device_id=(q * 2 + core, lax.rem(g + dz, NZ)), device_id_type=MESH
+            )
+            greeted += 1
     for copy in loads[1:]:
         copy.start()
 
@@ -162,7 +167,7 @@
         chip = chip_at(dx, dy)
         core = lax.rem(c + dc, 2)
         return pltpu.make_async_remote_copy(
-            src_ref=a_send.at[chip, core * 2 + lax.rem(parity + (s + dx + dy), 2)],
+            src_ref=a_send.at[chip, core * 2 + triple(0, s, dx + dy)],
             dst_ref=a_recv.at[s, b],
             send_sem=a_ssem.at[0, s],
             recv_sem=a_rsem.at[0, s],
@@ -176,7 +181,7 @@
                 for dc in range(2):
                     a_copy(s, dx, dy, dc).start()
             a_copy(s, 0, 0, 1).start()
-            a_recv[s, b] = a_send[q, c * 2 + lax.rem(parity + s, 2)]
+            a_recv[s, b] = a_send[q, c * 2 + triple(0, s)]
 
     def swap(p):
         return pltpu.make_async_remote_copy(
@@ -191,7 +196,7 @@
     def m_copy(p, s, dx, dy):
         chip = chip_at(dx, dy)
         return pltpu.make_async_remote_copy(
-            src_ref=m_send.at[p - 1, chip, lax.rem(parity + (s + dx + dy), 2)],
+            src_ref=m_send.at[p - 1, chip, triple(p, s, dx + dy)],
             dst_ref=m_recv.at[p - 1, s, q],
             send_sem=a_ssem.at[p, s],
             recv_sem=a_rsem.at[p, s],
@@ -205,7 +210,7 @@
         for s in range(2):
             for dx, dy in A_ORDER:
                 m_copy(p, s, dx, dy).start()
-            m_recv[p - 1, s, q] = m_send[p - 1, q, lax.rem(parity + s, 2)]
+            m_recv[p - 1, s, q] = m_send[p - 1, q, triple(p, s)]
 
     def a_all(p, s):
         if p == 0:
@@ -289,7 +294,7 @@
             z_send[p, z_rows(s, e)] = rows[e * block : (e + 1) * block].reshape(CHIPS, TRI, 128)
 
     def z_copy(p, s, e):
-        plane = (e >> 1) * 4 + 2 * c + lax.rem(parity + s, 2)
+        plane = (e >> 1) * 4 + 2 * c + triple(p, s)
         core = e & 1
         copy = pltpu.make_async_remote_copy(
             src_ref=z_send.at[p, z_rows(s, e)],
@@ -354,40 +359,45 @@
             device_id_type=MESH,
         )
 
-    def d_copy(p, s, e, dx, dy):
-        plane = (e >> 1) * 4 + 2 * c + lax.rem(parity + s, 2)
-        core = e & 1
+    def d_copy(p, s, order, core, dx, dy):
+        first = 2 * c + triple(p, s)
+        away = lax.rem(g - first + NZ, NZ)
+        far = jnp.where((away >= 2) & (away <= 6), 0, 1)
+        upper = lax.rem(far + order, 2)
         chip = chip_at(dx, dy)
+        row = (s * 4 + upper * 2 + core) * CHIPS + chip
+        plane = upper * 4 + first
         copy = pltpu.make_async_remote_copy(
-            src_ref=z_send.at[p, (s * 4 + e) * CHIPS + chip],
+            src_ref=z_send.at[p, row],
             dst_ref=out_ref.at[g, p, q],
             send_sem=z_ssem.at[p, s],
             recv_sem=b_rsem.at[p],
             device_id=(chip * 2 + core, plane),
             device_id_type=MESH,
         )
-        return copy, (plane == g) & (core == c)
+        return copy, row, (plane == g) & (core == c)
 
     def send_d(p, s):
-        for dx, dy in tuple(reversed(OFFSETS)):
-            for e in range(4):
-                d_copy(p, s, e, dx, dy)[0].start()
-        for e in range(4):
-            copy, here = d_copy(p, s, e, 0, 0)
-
-            @pl.when(jnp.logical_not(here))
-            def _():
-                copy.start()
-
-            @pl.when(here)
-            def _():
-                out_ref[g, p, q] = z_send[p, (s * 4 + e) * CHIPS + q]
-
-    def d_all(p, s, count):
+        for order in range(2):
+            for dx, dy in A_ORDER:
+                for core in range(2):
+                    d_copy(p, s, order, core, dx, dy)[0].start()
+            for core in range(2):
+                copy, row, here = d_copy(p, s, order, core, 0, 0)
+
+                @pl.when(jnp.logical_not(here))
+                def _():
+                    copy.start()
+
+                @pl.when(here)
+                def _():
+                    out_ref[g, p, q] = z_send[p, row]
+
+    def d_all(p, count):
         return pltpu.make_async_remote_copy(
             src_ref=z_send.at[p, pl.ds(0, count)],
             dst_ref=z_send.at[p, pl.ds(0, count)],
-            send_sem=z_ssem.at[p, s],
+            send_sem=z_ssem.at[p, 0],
             recv_sem=b_rsem.at[p],
             device_id=(b, g),
             device_id_type=MESH,
@@ -400,57 +410,50 @@
         def _():
             with jax.named_scope(f"wait_z#p={p}#s={s}"):
                 wait_z(p)
-            for dx, dy in reversed(OFFSETS):
+            for dx, dy in A_ORDER:
                 b_copy(p, dx, dy).start()
             out_ref[:, p, q] = z_recv[p, q]
 
+    final = PHASES - 1
     steps = [(p, s) for p in range(PHASES) for s in range(2)]
-    for k, step in enumerate(steps):
-        combine(*step)
-        with jax.named_scope(f"send_z#p={step[0]}#s={step[1]}"):
-            (send_d if step in DIRECT else send_z)(*step)
-        if k >= LAG and steps[k - LAG] not in DIRECT:
+    for k, (p, s) in enumerate(steps):
+        combine(p, s)
+        with jax.named_scope(f"send_z#p={p}#s={s}"):
+            if p < final:
+                send_z(p, s)
+            else:
+                send_d(p, s)
+        if k >= LAG:
             pass_on(*steps[k - LAG])
-    for step in steps[-LAG:]:
-        if step not in DIRECT:
-            pass_on(*step)
-
-    for p in range(PHASES):
-        for s in range(2):
-            a_all(p, s).wait_send()
-            own = in_class & (mine == s)
-            part = 1 if (p, s) in DIRECT else CHIPS
-
-            @pl.when(own)
-            def _():
-                blocks(p, s, 4 * CHIPS - part).wait_send()
-
-            @pl.when(jnp.logical_not(own))
-            def _():
-                blocks(p, s, 4 * CHIPS).wait_send()
+
+    for p, s in steps:
+        a_all(p, s).wait_send()
+        own = in_class & ((mine == s) if p < final else (s == 0))
+        part = CHIPS if p < final else 1
+
+        @pl.when(own)
+        def _():
+            blocks(p, s, 4 * CHIPS - part).wait_send()
+
+        @pl.when(jnp.logical_not(own))
+        def _():
+            blocks(p, s, 4 * CHIPS).wait_send()
 
     for p in range(1, PHASES):
         swap(p).wait_send()
-
-    for p in range(PHASES):
-        for s in range(2):
-
-            @pl.when(mine == s)
-            def _():
-                with jax.named_scope(f"wait_b#p={p}#s={s}"):
-                    if (p, s) in DIRECT:
-
-                        @pl.when(in_class)
-                        def _():
-                            d_all(p, s, NZ * CHIPS - 1).wait_recv()
-
-                        @pl.when(jnp.logical_not(in_class))
-                        def _():
-                            d_all(p, s, NZ * CHIPS).wait_recv()
-
-                    else:
-                        b_all(p).wait_recv()
-                        b_all(p).wait_send()
+    for p in range(final):
+        with jax.named_scope(f"wait_b#p={p}"):
+            b_all(p).wait_recv()
+            b_all(p).wait_send()
+    with jax.named_scope("wait_d"):
+
+        @pl.when(in_class)
+        def _():
+            d_all(final, NZ * CHIPS - 1).wait_recv()
+
+        @pl.when(jnp.logical_not(in_class))
+        def _():
+            d_all(final, NZ * CHIPS).wait_recv()
 
 
 def on_device(band_coeffs, sign_table, slice_widths, owner_map):

time: 38.8 us -> 38 us (0.979)
  Pallas kernels: 37.9 us -> 37.1 us
    pallas_call x1, Pallas kernels: 37.9 us -> 37.1 us  [on_device(): pl.pallas_call(kernel, out_shape=jax.ShapeDtypeStruct((NZ, PHASES, CHIPS,...]
where the time goes in v5:
time: 38 us; the launch traced here: 37.9 us
  Pallas kernels  37.1 us (98%)
  local copies, waits for them, and re-layouts  0.88 us (2%)
    pallas_call x1, Pallas kernels, on_device(): pl.pallas_call(kernel, out_shape=jax.ShapeDtypeStruct((NZ, PHASES, CHIPS,...  37.1 us
    unnamed x1, local copies, waits for them, and re-layouts  0.88 us

profile of v5, /device:TPU:1, one launch (start us, length us, event | category | flops | bytes accessed | tf_op | source)
XLA Modules:
  0.0 37.9 jit_solution(12754051965014980377)
XLA Ops:
  0.0 37.1 %pseudobands.1 = f32[8,3,16,3,128]{4,3,2,1,0:T(4,128)S(1)} custom-call(f32[384,6144]{1,0:T(8,128)} %band_ref.1, s32[12,384]{1,0:T(8,128)} %sign_ref.1, s32[1,64]{1,0:T(1,128)} %bitcast.8, s32[1,64]{1,0:T(1,128)} %bitcast.9), custom_call_target="tpu_custom_call" | custom-call | tf_op jit(solution)/shard_map/pseudobands/pallas_call | solution.py:463
  37.1 0.9 %copy.7 = f32[3,49152]{1,0:T(4,128)} copy(f32[3,49152]{1,0:T(4,128)S(1)} %bitcast.7) | data formatting | bytes 1179648

commit v6 on v5

--- a/solution.py
+++ b/solution.py
@@ -177,8 +177,8 @@
 
     def send_a():
         for s in range(2):
-            for dx, dy in A_ORDER:
-                for dc in range(2):
+            for dc in (1, 0):
+                for dx, dy in A_ORDER:
                     a_copy(s, dx, dy, dc).start()
             a_copy(s, 0, 0, 1).start()
             a_recv[s, b] = a_send[q, c * 2 + triple(0, s)]

time: 38 us -> 37.9 us (level)
  no operation moved by 1% of the time
where the time goes in v6:
time: 37.9 us
  Pallas kernels  37 us (98%)
  local copies, waits for them, and re-layouts  0.88 us (2%)
    pallas_call x1, Pallas kernels, on_device(): pl.pallas_call(kernel, out_shape=jax.ShapeDtypeStruct((NZ, PHASES, CHIPS,...  37 us
    unnamed x1, local copies, waits for them, and re-layouts  0.88 us

profile of v6, /device:TPU:1, one launch (start us, length us, event | category | flops | bytes accessed | tf_op | source)
XLA Modules:
  0.0 37.9 jit_solution(16076070349829138022)
XLA Ops:
  0.0 37.0 %pseudobands.1 = f32[8,3,16,3,128]{4,3,2,1,0:T(4,128)S(1)} custom-call(f32[384,6144]{1,0:T(8,128)} %band_ref.1, s32[12,384]{1,0:T(8,128)} %sign_ref.1, s32[1,64]{1,0:T(1,128)} %bitcast.8, s32[1,64]{1,0:T(1,128)} %bitcast.9), custom_call_target="tpu_custom_call" | custom-call | tf_op jit(solution)/shard_map/pseudobands/pallas_call | solution.py:463
  37.0 0.9 %copy.7 = f32[3,49152]{1,0:T(4,128)} copy(f32[3,49152]{1,0:T(4,128)S(1)} %bitcast.7) | data formatting | bytes 1179648
